TPU v7x, 32 devices: a whole 2x2x4 slice. The times are simulated.
32 devices in a mesh: row: 4 (over z), col: 8 (over y, x, core).
Axes of the slice: x: 2, y: 2, z: 4, core: 2. Of those that a mesh axis runs over, the one named last changes fastest.
Arguments:
- train_points: float32 [4, 32, 4096], P('row', None, 'col'), as said below
- targets: float32 [4, 4096], P('row', 'col'), may hold values from -16 to 16
- inverse_factor: float32 [4, 4096, 1024], P('row', 'col')
- counts: int32 [4, 4], P('row'), may hold values from 512 to 1024, as said below
- membership: int32 [4, 4, 16], replicated, may hold values from 0 to 1, as said below
- test_points: float32 [16, 32, 128], P('row'), may hold values from -6 to 6
Outputs:
- pred_mean: float32 [16, 128], P('row')
- pred_var: float32 [16, 128], P('row')
Inputs may be any that keep to these rules, and one draw needn't show every extreme that they name: Each expert membership[r, c, :] takes part in at least one and at most 4 blocks, exactly 4 for at least one expert, and in at most one of the 4 blocks of each owner row. `counts`: at least one expert has all 1024 points valid. `train_points`: each expert's 1024 points are drawn independently of the other experts' points.
All inputs are finite; a program needn't handle non-finite values.
Results may differ from a plain program's by a relative error of at most 0.0003.
Values sent between devices are 32-bit elements; how exact they have to be, the bound alone decides.
A program may use at most 64 MiB of HBM per device.

v0:
```python
import jax
import jax.numpy as jnp
from jax import lax
from jax.sharding import PartitionSpec as P

SIGNAL = 1.0
NOISE = 0.1
HIGHEST = lax.Precision.HIGHEST


def partner_2(block, axis, distance):
    count = lax.axis_size(axis)
    route = []
    for low in range(count):
        high = low | 1 << distance
        if high != low and high < count:
            route += [(low, high), (high, low)]
    return lax.ppermute(block, axis, route)


def cross_kernel(train_cols, test_cols, squared_scale):
    products = jnp.einsum("dn,dp->np", train_cols, test_cols, precision=HIGHEST)
    spread = (
        jnp.sum(train_cols * train_cols, axis=0)[:, None]
        + jnp.sum(test_cols * test_cols, axis=0)[None, :]
        - 2.0 * products
    )
    return SIGNAL * jnp.exp(-0.5 * spread / squared_scale)


def slot_table(member, slot_count):
    before = jnp.cumsum(member) - member
    slot_ids = jnp.arange(slot_count, dtype=jnp.int32)[:, None]
    picked = ((member[None, :] == 1) & (before[None, :] == slot_ids)).astype(jnp.int32)
    chosen = jnp.sum(picked * jnp.arange(member.shape[0], dtype=jnp.int32)[None, :], axis=1)
    return (picked.astype(jnp.float32), chosen)


def weigh_expert(mean_part, quad_part):
    variance = NOISE + jnp.maximum(SIGNAL - quad_part, 0.0)
    entropy_gap = 0.5 * (jnp.log(SIGNAL + NOISE) - jnp.log(variance))
    weight = entropy_gap / variance
    return (weight * mean_part, weight)


def on_device(train_points, targets, inverse_factor, counts, membership, test_points):
    parity = lax.axis_index("col") % 2
    expert_col = lax.axis_index("col") // 2
    own_row = lax.axis_index("row")
    row_count = lax.axis_size("row")
    slot_count = min(8, row_count)
    features = train_points.shape[1]
    rows_half = train_points.shape[2]
    blocks_own = test_points.shape[0]
    block_len = test_points.shape[2]
    squared_scale = 0.5 * features
    own_points = train_points[0]
    own_targets = targets[0]
    packed = jnp.concatenate([own_points, own_targets[None, :]], axis=0)
    partner = partner_2(packed, "col", 0)
    other_points = partner[:features]
    other_targets = partner[features]
    member = membership[own_row, expert_col]
    picked, chosen = slot_table(member, slot_count)
    wanted = lax.dynamic_slice_in_dim(
        membership[:, expert_col], own_row * blocks_own, blocks_own, 1
    )
    gathered = lax.all_gather(test_points, "row", axis=0, tiled=True)
    slot_tests = gathered[chosen]
    test_cols = slot_tests.transpose(1, 0, 2).reshape(features, slot_count * block_len)
    valid_count = counts[0, expert_col]
    local_index = jnp.arange(rows_half, dtype=jnp.int32)
    own_valid = 2 * local_index + parity < valid_count
    other_valid = 2 * local_index + (1 - parity) < valid_count
    own_kernel = jnp.where(
        own_valid[:, None], cross_kernel(own_points, test_cols, squared_scale), 0.0
    )
    other_kernel = jnp.where(
        other_valid[:, None], cross_kernel(other_points, test_cols, squared_scale), 0.0
    )
    factor_pairs = inverse_factor[0].reshape(rows_half, rows_half, 2)
    own_part = lax.dynamic_index_in_dim(factor_pairs, parity, 2, keepdims=False)
    other_part = lax.dynamic_index_in_dim(factor_pairs, 1 - parity, 2, keepdims=False)
    solved = jnp.dot(own_part, own_kernel, precision=HIGHEST, preferred_element_type=jnp.float32)
    solved = solved + jnp.dot(
        other_part, other_kernel, precision=HIGHEST, preferred_element_type=jnp.float32
    )
    whitened = jnp.dot(own_part, own_targets, precision=HIGHEST, preferred_element_type=jnp.float32)
    whitened = whitened + jnp.dot(
        other_part, other_targets, precision=HIGHEST, preferred_element_type=jnp.float32
    )
    mean_own = jnp.dot(whitened, solved, precision=HIGHEST, preferred_element_type=jnp.float32)
    quad_own = jnp.sum(solved * solved, axis=0)
    partials = partner_2(jnp.stack([mean_own, quad_own], axis=0), "col", 0)
    weighted, weight = weigh_expert(mean_own + partials[0], quad_own + partials[1])
    slot_ids = jnp.arange(slot_count, dtype=jnp.int32)
    my_slots = (slot_ids % 2 == parity).astype(jnp.float32)[:, None]
    my_picked = picked * my_slots
    dense_num = jnp.einsum(
        "sb,sp->bp", my_picked, weighted.reshape(slot_count, block_len), precision=HIGHEST
    )
    dense_wgt = jnp.einsum(
        "sb,sp->bp", my_picked, weight.reshape(slot_count, block_len), precision=HIGHEST
    )
    row_num = jnp.sum(dense_num.reshape(row_count, blocks_own, block_len), axis=1)
    row_wgt = jnp.sum(dense_wgt.reshape(row_count, blocks_own, block_len), axis=1)
    outgoing_sums = jnp.stack([row_num, row_wgt], axis=1)
    arrived = lax.all_to_all(outgoing_sums, "row", split_axis=0, concat_axis=0, tiled=True)
    placed = jnp.einsum("rj,rkp->kjp", wanted.astype(jnp.float32), arrived, precision=HIGHEST)
    total_num, total_wgt = lax.psum((placed[0], placed[1]), "col")
    precision_sum = 1.0 / (SIGNAL + NOISE) + total_wgt
    return (total_num / precision_sum, 1.0 / precision_sum)


def solution(mesh):
    in_specs = (
        P("row", None, "col"),
        P("row", "col"),
        P("row", "col", None),
        P("row", None),
        P(),
        P("row", None, None),
    )
    out_specs = (P("row", None), P("row", None))
    return jax.shard_map(
        on_device, mesh=mesh, in_specs=in_specs, out_specs=out_specs, check_vma=False
    )
```

profile of v0, /device:TPU:0, one launch (start us, length us, event | category | flops | bytes accessed | tf_op | source)
XLA Modules:
  0.0 70.3 jit_solution(5931016102477284509)
XLA Ops:
  0.6 0.0 copy-start
  0.6 0.9 %pad_maximum_fusion = f32[33,512]{1,0:T(8,128)S(1)} fusion(f32[1,512]{1,0:T(1,128)} %param.7, f32[32,512]{1,0:T(8,128)} %bitcast.99), kind=kLoop, calls=%fused_computation.30 | loop fusion | flops 16896 | bytes 135168 | tf_op jit(solution)/shard_map/concatenate | solution.py:59
  1.5 0.5 collective-permute-start
  2.0 0.9 %multiply_reduce_fusion.2 = f32[512]{0:T(512)S(1)} fusion(f32[1,32,512]{2,1,0:T(8,128)} %param.6), kind=kLoop, calls=%fused_computation.36 | loop fusion | flops 32256 | bytes 67584 | tf_op jit(solution)/shard_map/reduce_sum | solution.py:24
  2.9 3.0 %copy.30 = f32[1,512,1024]{1,2,0:T(8,128)} copy(f32[1,512,1024]{2,1,0:T(8,128)} %param.8) | data formatting | bytes 4194304 | tf_op args[2]
  5.8 2.5 %reshape_squeeze.3 = f32[512,512,2]{0,2,1:T(2,128)S(1)} reshape(f32[1,512,1024]{1,2,0:T(8,128)} %copy.30) | data formatting | bytes 4194304 | tf_op jit(solution)/shard_map/reshape;squeeze | solution.py:81
  8.3 2.8 %constant_dynamic-slice_fusion = (f32[512,512,1]{0,2,1:T(1,128)}, f32[512,512,1]{0,2,1:T(1,128)S(1)}) fusion(f32[512,512,2]{0,2,1:T(2,128)S(1)} %reshape_squeeze.3, s32[]{:T(128)S(6)} %select_n.68, s32[]{:T(128)S(6)} %select_n.65), kind=kLoop, calls=%fused_computation.76 | loop fusion | bytes 4194312 | tf_op jit(solution)/shard_map/jit(dynamic_index_in_dim)/dynamic_slice | solution.py:83
  11.1 0.0 copy-start.3
  11.1 2.4 %copy.34 = f32[512,512,1]{1,0,2:T(8,128)S(1)} copy(f32[512,512,1]{0,2,1:T(1,128)} %get-tuple-element.6) | data formatting | bytes 2097152 | tf_op jit(solution)/shard_map/jit(dynamic_index_in_dim)/dynamic_slice | solution.py:83
  13.5 0.0 copy-start.2
  13.5 0.0 copy-start.1
  13.5 1.3 %copy.31 = f32[512,512,1]{1,0,2:T(8,128)S(1)} copy(f32[512,512,1]{0,2,1:T(1,128)S(1)} %get-tuple-element.7) | data formatting | bytes 2097152 | tf_op jit(solution)/shard_map/jit(dynamic_index_in_dim)/dynamic_slice | solution.py:82
  14.8 0.0 copy-done.3
  14.8 1.0 %fusion.8 = f32[1,512]{1,0:T(1,128)S(1)} fusion(f32[512,512,1]{1,0,2:T(8,128)S(1)} %copy.31, f32[1,512]{1,0:T(1,128)S(1)} %copy-done.3), kind=kOutput, calls=%fused_computation.15 | convolution fusion | flops 3145728 | bytes 1052672 | tf_op jit(solution)/shard_map/dot_general | solution.py:88
  15.8 0.7 %bitcast_compare_fusion = (pred[16]{0:T(512)(128)(4,1)S(1)}, s32[1,1,16]{2,1,0:T(1,128)S(1)}) fusion(s32[4,4,16]{2,1,0:T(4,128)} %param.10, s32[]{:T(128)S(6)} %select_n.60, s32[]{:T(128)S(6)} %select_n.62), kind=kLoop, calls=%fused_computation.83 | loop fusion | flops 16 | bytes 152 | tf_op jit(solution)/shard_map/eq | solution.py:34
  16.5 0.1 copy.29
  16.7 0.1 reduce.2
  16.8 0.1 select_reduce_fusion
  16.9 0.0 copy-done.2
  16.9 15.2 %all_gather.3 = f32[16,32,128]{2,1,0:T(8,128)S(1)} all-gather(f32[4,32,128]{2,1,0:T(8,128)S(1)} %copy-done.2), channel_id=1, replica_groups=mesh['row'=4,'col'=8] {'row'}, dimensions={0}, use_global_device_ids=true | all-gather | bytes 327680 | tf_op jit(solution)/shard_map/all_gather | solution.py:68
  32.2 0.6 gather_fusion
  32.8 0.0 copy-done
  32.8 0.6 constant_dynamic-slice_fusion.1
  33.4 0.7 add_compare_fusion.1
  34.0 0.0 copy-done.1
  34.0 1.2 %fusion.4 = f32[512,512]{0,1:T(8,128)S(1)} fusion(f32[512]{0:T(512)S(1)} %bitcast.101, f32[512]{0:T(512)S(1)} %multiply_reduce_fusion.2, pred[512]{0:T(512)(128)(4,1)S(1)} %add_compare_fusion.1, f32[1,32,512]{2,1,0:T(8,128)S(1)} %copy-done.1, f32[4,32,128]{2,1,0:T(8,128)S(1)} %gather_fusion), kind=kOutput, calls=%fused_computation.8 | convolution fusion | flops 101974016 | bytes 1184256 | tf_op jit(solution)/shard_map/dn,dp->np/dot_general | solution.py:22
  35.2 1.9 %fusion.10 = f32[512,512]{1,0:T(8,128)S(1)} fusion(f32[512,512]{0,1:T(8,128)S(1)} %fusion.4, f32[512,512,1]{1,0,2:T(8,128)S(1)} %copy.31), kind=kOutput, calls=%fused_computation.17 | convolution fusion | flops 1610612736 | bytes 3145728 | tf_op jit(solution)/shard_map/dot_general | solution.py:84
  37.1 0.5 broadcast.207
  37.6 0.7 reduce.6
  38.3 0.1 broadcast_in_dim_squeeze.5
  38.4 0.7 add_compare_fusion
  39.1 0.0 collective-permute-done
  39.1 1.0 %fusion.5 = f32[1,512]{1,0:T(1,128)S(1)} fusion(f32[512,512,1]{1,0,2:T(8,128)S(1)} %copy.34, f32[33,512]{1,0:T(8,128)S(1)} %collective-permute-done), kind=kOutput, calls=%fused_computation.12 | convolution fusion | flops 3145728 | bytes 1052672 | tf_op jit(solution)/shard_map/dot_general | solution.py:89
  40.1 1.0 %convolution_multiply_fusion = f32[512,512]{0,1:T(8,128)S(1)} fusion(f32[33,512]{1,0:T(8,128)S(1)} %collective-permute-done, f32[4,32,128]{2,1,0:T(8,128)S(1)} %gather_fusion), kind=kOutput, calls=%fused_computation.2 | convolution fusion | flops 100925440 | bytes 1179648 | tf_op jit(solution)/shard_map/dn,dp->np/dot_general | solution.py:22
  41.1 2.1 %multiply_reduce_fusion = (f32[512]{0:T(512)S(1)}, f32[512,512]{1,0:T(8,128)S(1)}) fusion(f32[512,512]{1,0:T(8,128)S(1)} %fusion.10, f32[512,512]{0,1:T(8,128)S(1)} %convolution_multiply_fusion, f32[512]{0:T(512)S(1)} %multiply_reduce_fusion.1, f32[512]{0:T(512)S(1)} %bitcast.102, pred[512]{0:T(512)(128)(4,1)S(1)} %add_compare_fusion, ...), kind=kOutput, calls=%fused_computation.19 | convolution fusion | flops 1612447232 | bytes 4200960 | tf_op jit(solution)/shard_map/dot_general | solution.py:85
  43.3 0.6 fusion.51
  43.9 0.1 collective-permute-start.1
  44.0 0.1 reshape.144
  44.1 1.1 %collective-permute-done.1 = f32[2,512]{1,0:T(2,128)S(1)} collective-permute-done((f32[2,512]{1,0:T(2,128)S(1)}, f32[2,512]{1,0:T(2,128)S(1)}, u32[]{:S(2)}, u32[]{:S(2)}) %collective-permute-start.1) | collective-permute-done | bytes 4128 | tf_op jit(solution)/shard_map/ppermute | solution.py:18
  45.1 0.3 convolution_reduce_fusion
  45.4 0.3 convolution_reduce_fusion.1
  45.6 0.6 pad_maximum_fusion.2
  46.3 5.2 %all-to-all-start = ((f32[4,2,128]{2,1,0:T(2,128)}), f32[4,2,128]{2,1,0:T(2,128)S(1)}, u32[]{:S(2)}, u32[]{:S(2)}) async-start(f32[4,2,128]{2,1,0:T(2,128)} %pad_maximum_fusion.2), calls=%async_computation | async-start | bytes 8192 | tf_op jit(solution)/shard_map/all_to_all | solution.py:108
  51.4 0.8 %dynamic-slice_convert_fusion = f32[4,1,4]{2,1,0:T(1,128)S(1)} fusion(s32[4,4,16]{2,1,0:T(4,128)} %param.10, s32[]{:T(128)S(6)} %select_n.70, s32[]{:T(128)S(6)} %select_n.72), kind=kLoop, calls=%fused_computation.62 | loop fusion | flops 16 | bytes 136 | tf_op jit(solution)/shard_map/convert_element_type | solution.py:109
  52.2 4.8 %all-to-all-done = f32[4,2,128]{2,1,0:T(2,128)S(1)} async-done(((f32[4,2,128]{2,1,0:T(2,128)}), f32[4,2,128]{2,1,0:T(2,128)S(1)}, u32[]{:S(2)}, u32[]{:S(2)}) %all-to-all-start) | async-done | bytes 4128 | tf_op jit(solution)/shard_map/all_to_all | solution.py:108
  57.0 0.2 convolution_bitcast_fusion
  57.2 12.6 %all-reduce = (f32[4,128]{1,0:T(4,128)S(1)}, f32[4,128]{1,0:T(4,128)S(1)}) all-reduce(f32[4,128]{1,0:T(4,128)S(1)} %get-tuple-element.9, f32[4,128]{1,0:T(4,128)S(1)} %get-tuple-element.8), channel_id=1, replica_groups=mesh['row'=4,'col'=8] {'col'}, use_global_device_ids=true, to_apply=%region_8.9 | all-reduce | flops 1024 | bytes 8192 | tf_op jit(solution)/shard_map/psum | solution.py:110
  69.7 0.6 add_divide_fusion
  (13 shorter events, 0.2 us)
Async XLA Ops:
  0.6 32.1 %copy-start = (s32[1,4]{1,0:T(1,128)S(1)}, s32[1,4]{1,0:T(1,128)}, u32[]{:S(2)}) copy-start(s32[1,4]{1,0:T(1,128)} %param.9) | copy-start | bytes 52
  1.5 37.5 %collective-permute-start = (f32[33,512]{1,0:T(8,128)S(1)}, f32[33,512]{1,0:T(8,128)S(1)}, u32[]{:S(2)}, u32[]{:S(2)}) collective-permute-start(f32[33,512]{1,0:T(8,128)S(1)} %pad_maximum_fusion), channel_id=1, source_target_pairs={{0,1},{1,0},{2,3},{3,2},{4,5},{5,4},{6,7},{7,6},{8,9},{9,8},{10,11... | collective-permute-start | bytes 202760 | tf_op jit(solution)/shard_map/ppermute | solution.py:18
  11.1 3.7 %copy-start.3 = (f32[1,512]{1,0:T(1,128)S(1)}, f32[1,512]{1,0:T(1,128)}, u32[]{:S(2)}) copy-start(f32[1,512]{1,0:T(1,128)} %param.7) | copy-start | bytes 6148
  13.5 3.4 %copy-start.2 = (f32[4,32,128]{2,1,0:T(8,128)S(1)}, f32[4,32,128]{2,1,0:T(8,128)}, u32[]{:S(2)}) copy-start(f32[4,32,128]{2,1,0:T(8,128)} %param.11) | copy-start | bytes 196612
  13.5 20.5 %copy-start.1 = (f32[1,32,512]{2,1,0:T(8,128)S(1)}, f32[1,32,512]{2,1,0:T(8,128)}, u32[]{:S(2)}) copy-start(f32[1,32,512]{2,1,0:T(8,128)} %param.6) | copy-start | bytes 196612
  43.9 1.2 %collective-permute-start.1 = (f32[2,512]{1,0:T(2,128)S(1)}, f32[2,512]{1,0:T(2,128)S(1)}, u32[]{:S(2)}, u32[]{:S(2)}) collective-permute-start(f32[2,512]{1,0:T(2,128)S(1)} %pad_maximum_fusion.1), channel_id=1, source_target_pairs={{0,1},{1,0},{2,3},{3,2},{4,5},{5,4},{6,7},{7,6},{8,9},{9,8},{10,11... | collective-permute-start | bytes 12296 | tf_op jit(solution)/shard_map/ppermute | solution.py:18
  46.3 10.7 %all-to-all-start = ((f32[4,2,128]{2,1,0:T(2,128)}), f32[4,2,128]{2,1,0:T(2,128)S(1)}, u32[]{:S(2)}, u32[]{:S(2)}) async-start(f32[4,2,128]{2,1,0:T(2,128)} %pad_maximum_fusion.2), calls=%async_computation | async-start | bytes 8192 | tf_op jit(solution)/shard_map/all_to_all | solution.py:108
where the time goes:
time: 70.8 us; the launch traced here: 70.3 us
  blocking collectives  27.8 us (39%)
  local copies, waits for them, and re-layouts  13.8 us (19%)
  matrix products  9.53 us (13%)
  other arithmetic  6.76 us (10%)
  waiting for transfers between devices  5.86 us (8%)
  starting transfers between devices  5.72 us (8%)
  between operations  0.83 us (1%)
    all_gather x1, blocking collectives, on_device(): gathered = lax.all_gather(test_points, 'row', axis=0, tiled=True)  15.2 us
    psum x1, blocking collectives, on_device(): total_num, total_wgt = lax.psum((placed[0], placed[1]), 'col')  12.6 us
    all_to_all x1, starting transfers between devices, on_device(): lax.all_to_all(outgoing_sums, 'row', split_axis=0, concat_axis=0, tiled=T...  5.16 us
    dynamic_slice x2, local copies, waits for them, and re-layouts, on_device(): lax.dynamic_index_in_dim(factor_pairs, 1 - parity, 2, keepdims=False)  5.15 us
    all_to_all x1, waiting for transfers between devices, on_device(): lax.all_to_all(outgoing_sums, 'row', split_axis=0, concat_axis=0, tiled=T...  4.81 us
    unnamed x9, local copies, waits for them, and re-layouts  2.98 us
    another operation x1, local copies, waits for them, and re-layouts, on_device(): factor_pairs = inverse_factor[0].reshape(rows_half, rows_half, 2)  2.49 us
    dot_general x2, matrix products, cross_kernel(): products = jnp.einsum('dn,dp->np', train_cols, test_cols, precision=HIGHEST)  2.25 us
  transfers between devices with their start and end apart: 3, of which 2 were waited for; matrix products, arithmetic and copies ran while one was open for 32% of the time, Pallas kernels for 0%

commit v1 on v0

--- a/solution.py
+++ b/solution.py
@@ -6,6 +6,16 @@
 SIGNAL = 1.0
 NOISE = 0.1
 HIGHEST = lax.Precision.HIGHEST
+
+
+def around_the_ring(x, axis, dim):
+    size = lax.axis_size(axis)
+    block, blocks = (x, [x])
+    for _ in range(size - 1):
+        block = lax.ppermute(block, axis, [(i, (i + 1) % size) for i in range(size)])
+        blocks.insert(0, block)
+    flat = jnp.concatenate(blocks, axis=dim)
+    return jnp.roll(flat, (lax.axis_index(axis) + 1) * x.shape[dim], axis=dim)
 
 
 def partner_2(block, axis, distance):
@@ -65,7 +75,7 @@
     wanted = lax.dynamic_slice_in_dim(
         membership[:, expert_col], own_row * blocks_own, blocks_own, 1
     )
-    gathered = lax.all_gather(test_points, "row", axis=0, tiled=True)
+    gathered = around_the_ring(test_points, "row", 0)
     slot_tests = gathered[chosen]
     test_cols = slot_tests.transpose(1, 0, 2).reshape(features, slot_count * block_len)
     valid_count = counts[0, expert_col]

time: 70.8 us -> 68.1 us (0.962)
  blocking collectives: 27.8 us -> 12.8 us
  waiting for transfers between devices: 5.86 us -> 15.5 us
  starting transfers between devices: 5.72 us -> 8.06 us
    all_gather x1 -> x0, blocking collectives: 15.2 us -> none  [on_device(): gathered = lax.all_gather(test_points, 'row', axis=0, tiled=True)]
    ppermute x0 -> x3, waiting for transfers between devices: none -> 9.73 us  [around_the_ring(): lax.ppermute(block, axis, [(i, (i + 1) % size) for i in range(size)])]
    ppermute x0 -> x3, starting transfers between devices: none -> 4.74 us  [around_the_ring(): lax.ppermute(block, axis, [(i, (i + 1) % size) for i in range(size)])]
    all_to_all x1, starting transfers between devices: 5.16 us -> 3.24 us  [on_device(): lax.all_to_all(outgoing_sums, 'row', split_axis=0, concat_axis=0, tiled=T...]
    dynamic_slice x2, local copies, waits for them, and re-layouts: 5.15 us -> 4.1 us  [on_device(): lax.dynamic_index_in_dim(factor_pairs, 1 - parity, 2, keepdims=False)]
    dynamic_slice x1, local copies, waits for them, and re-layouts: 1.31 us -> 2.36 us  [on_device(): own_part = lax.dynamic_index_in_dim(factor_pairs, parity, 2, keepdims=False)]
    unnamed x9 -> x16, local copies, waits for them, and re-layouts: 2.98 us -> 3.02 us
  transfers between devices with their start and end apart: 3 -> 6, of which waited for: 2 -> 4; matrix products, arithmetic and copies ran while one was open for 32% -> 31% of each run, Pallas kernels for 0% -> 0%
where the time goes in v1:
time: 68.1 us; the launch traced here: 67.6 us
  waiting for transfers between devices  15.5 us (23%)
  local copies, waits for them, and re-layouts  13.9 us (20%)
  blocking collectives  12.8 us (19%)
  matrix products  9.51 us (14%)
  starting transfers between devices  8.06 us (12%)
  other arithmetic  6.75 us (10%)
  between operations  0.96 us (1%)
    psum x1, blocking collectives, on_device(): total_num, total_wgt = lax.psum((placed[0], placed[1]), 'col')  12.8 us
    ppermute x3, waiting for transfers between devices, around_the_ring(): lax.ppermute(block, axis, [(i, (i + 1) % size) for i in range(size)])  9.73 us
    all_to_all x1, waiting for transfers between devices, on_device(): lax.all_to_all(outgoing_sums, 'row', split_axis=0, concat_axis=0, tiled=T...  4.77 us
    ppermute x3, starting transfers between devices, around_the_ring(): lax.ppermute(block, axis, [(i, (i + 1) % size) for i in range(size)])  4.74 us
    dynamic_slice x2, local copies, waits for them, and re-layouts, on_device(): lax.dynamic_index_in_dim(factor_pairs, 1 - parity, 2, keepdims=False)  4.1 us
    all_to_all x1, starting transfers between devices, on_device(): lax.all_to_all(outgoing_sums, 'row', split_axis=0, concat_axis=0, tiled=T...  3.24 us
    unnamed x16, local copies, waits for them, and re-layouts  3.02 us
    another operation x1, local copies, waits for them, and re-layouts, on_device(): factor_pairs = inverse_factor[0].reshape(rows_half, rows_half, 2)  2.49 us
  transfers between devices with their start and end apart: 6, of which 4 were waited for; matrix products, arithmetic and copies ran while one was open for 31% of the time, Pallas kernels for 0%

profile of v1, /device:TPU:0, one launch (start us, length us, event | category | flops | bytes accessed | tf_op | source)
XLA Modules:
  0.0 67.6 jit_solution(6687823850879580918)
XLA Ops:
  0.6 0.0 copy-start
  0.6 3.1 %collective-permute-start = (f32[4,32,128]{2,1,0:T(8,128)}, f32[4,32,128]{2,1,0:T(8,128)S(1)}, u32[]{:S(2)}, u32[]{:S(2)}) collective-permute-start(f32[4,32,128]{2,1,0:T(8,128)} %param.11), channel_id=1, source_target_pairs={{0,8},{8,16},{16,24},{24,0},{1,9},{9,17},{17,25},{25,1},{2,10},{10... | collective-permute-start | bytes 196616 | tf_op jit(solution)/shard_map/ppermute | solution.py:15
  3.7 0.9 %pad_maximum_fusion = f32[33,512]{1,0:T(8,128)S(1)} fusion(f32[1,512]{1,0:T(1,128)} %param.7, f32[32,512]{1,0:T(8,128)} %bitcast.99), kind=kLoop, calls=%fused_computation.30 | loop fusion | flops 16896 | bytes 135168 | tf_op jit(solution)/shard_map/concatenate | solution.py:69
  4.6 0.0 collective-permute-start.3
  4.7 0.9 %multiply_reduce_fusion.2 = f32[512]{0:T(512)S(1)} fusion(f32[1,32,512]{2,1,0:T(8,128)} %param.6), kind=kLoop, calls=%fused_computation.36 | loop fusion | flops 32256 | bytes 67584 | tf_op jit(solution)/shard_map/reduce_sum | solution.py:34
  5.5 3.0 %copy.30 = f32[1,512,1024]{1,2,0:T(8,128)} copy(f32[1,512,1024]{2,1,0:T(8,128)} %param.8) | data formatting | bytes 4194304 | tf_op args[2]
  8.5 2.5 %reshape_squeeze.3 = f32[512,512,2]{0,2,1:T(2,128)S(1)} reshape(f32[1,512,1024]{1,2,0:T(8,128)} %copy.30) | data formatting | bytes 4194304 | tf_op jit(solution)/shard_map/reshape;squeeze | solution.py:91
  11.0 2.8 %constant_dynamic-slice_fusion = (f32[512,512,1]{0,2,1:T(1,128)S(1)}, f32[512,512,1]{0,2,1:T(1,128)}) fusion(f32[512,512,2]{0,2,1:T(2,128)S(1)} %reshape_squeeze.3, s32[]{:T(128)S(6)} %select_n.82, s32[]{:T(128)S(6)} %select_n.77), kind=kLoop, calls=%fused_computation.84 | loop fusion | bytes 4194312 | tf_op jit(solution)/shard_map/jit(dynamic_index_in_dim)/dynamic_slice | solution.py:93
  13.8 2.4 %copy.31 = f32[512,512,1]{1,0,2:T(8,128)S(1)} copy(f32[512,512,1]{0,2,1:T(1,128)} %get-tuple-element.7) | data formatting | bytes 2097152 | tf_op jit(solution)/shard_map/jit(dynamic_index_in_dim)/dynamic_slice | solution.py:92
  16.2 0.7 %bitcast_compare_fusion = (pred[16]{0:T(512)(128)(4,1)S(1)}, s32[1,1,16]{2,1,0:T(1,128)S(1)}) fusion(s32[4,4,16]{2,1,0:T(4,128)} %param.10, s32[]{:T(128)S(6)} %select_n.72, s32[]{:T(128)S(6)} %select_n.74), kind=kLoop, calls=%fused_computation.92 | loop fusion | flops 16 | bytes 152 | tf_op jit(solution)/shard_map/eq | solution.py:44
  16.9 0.1 copy.29
  17.0 0.1 reduce.2
  17.1 0.1 select_reduce_fusion
  17.3 0.6 constant_dynamic-slice_fusion.2
  17.8 0.7 add_compare_fusion.1
  18.5 0.0 copy-start.2
  18.5 1.3 %copy.34 = f32[512,512,1]{1,0,2:T(8,128)S(1)} copy(f32[512,512,1]{0,2,1:T(1,128)S(1)} %get-tuple-element.6) | data formatting | bytes 2097152 | tf_op jit(solution)/shard_map/jit(dynamic_index_in_dim)/dynamic_slice | solution.py:93
  19.8 0.0 copy-start.1
  19.9 1.0 %fusion.8 = f32[1,512]{1,0:T(1,128)S(1)} fusion(f32[512,512,1]{1,0,2:T(8,128)S(1)} %copy.31, f32[1,512]{1,0:T(1,128)S(1)} %copy-done.3), kind=kOutput, calls=%fused_computation.15 | convolution fusion | flops 3145728 | bytes 1052672 | tf_op jit(solution)/shard_map/dot_general | solution.py:98
  20.8 0.5 broadcast.208
  21.4 0.7 reduce.6
  22.0 0.1 broadcast_in_dim_squeeze.5
  22.1 0.7 add_compare_fusion
  22.8 0.0 collective-permute-done
  22.8 1.6 %collective-permute-start.1 = (f32[4,32,128]{2,1,0:T(8,128)S(1)}, f32[4,32,128]{2,1,0:T(8,128)S(1)}, u32[]{:S(2)}, u32[]{:S(2)}) collective-permute-start(f32[4,32,128]{2,1,0:T(8,128)S(1)} %collective-permute-done), channel_id=1, source_target_pairs={{0,8},{8,16},{16,24},{24,0},{1,9},{9,17},{17,25},{25,1},{2,10},{10... | collective-permute-start | bytes 196616 | tf_op jit(solution)/shard_map/ppermute | solution.py:15
  24.4 0.0 collective-permute-done.3
  24.4 1.0 %fusion.5 = f32[1,512]{1,0:T(1,128)S(1)} fusion(f32[512,512,1]{1,0,2:T(8,128)S(1)} %copy.34, f32[33,512]{1,0:T(8,128)S(1)} %collective-permute-done.3), kind=kOutput, calls=%fused_computation.12 | convolution fusion | flops 3145728 | bytes 1052672 | tf_op jit(solution)/shard_map/dot_general | solution.py:99
  25.4 3.7 %collective-permute-done.1 = f32[4,32,128]{2,1,0:T(8,128)S(1)} collective-permute-done((f32[4,32,128]{2,1,0:T(8,128)S(1)}, f32[4,32,128]{2,1,0:T(8,128)S(1)}, u32[]{:S(2)}, u32[]{:S(2)}) %collective-permute-start.1) | collective-permute-done | bytes 65568 | tf_op jit(solution)/shard_map/ppermute | solution.py:15
  29.1 0.0 collective-permute-start.2
  29.1 6.0 %collective-permute-done.2 = f32[4,32,128]{2,1,0:T(8,128)S(1)} collective-permute-done((f32[4,32,128]{2,1,0:T(8,128)S(1)}, f32[4,32,128]{2,1,0:T(8,128)S(1)}, u32[]{:S(2)}, u32[]{:S(2)}) %collective-permute-start.2) | collective-permute-done | bytes 65568 | tf_op jit(solution)/shard_map/ppermute | solution.py:15
  35.3 0.6 gather_fusion
  35.9 1.2 %fusion.4 = f32[512,512]{0,1:T(8,128)S(1)} fusion(f32[512]{0:T(512)S(1)} %bitcast.102, f32[512]{0:T(512)S(1)} %multiply_reduce_fusion.2, pred[512]{0:T(512)(128)(4,1)S(1)} %add_compare_fusion.1, f32[1,32,512]{2,1,0:T(8,128)S(1)} %copy-done.1, f32[4,32,128]{2,1,0:T(8,128)S(1)} %gather_fusion), kind=kOutput, calls=%fused_computation.8 | convolution fusion | flops 101974016 | bytes 1184256 | tf_op jit(solution)/shard_map/dn,dp->np/dot_general | solution.py:32
  37.1 1.9 %fusion.10 = f32[512,512]{1,0:T(8,128)S(1)} fusion(f32[512,512]{0,1:T(8,128)S(1)} %fusion.4, f32[512,512,1]{1,0,2:T(8,128)S(1)} %copy.31), kind=kOutput, calls=%fused_computation.17 | convolution fusion | flops 1610612736 | bytes 3145728 | tf_op jit(solution)/shard_map/dot_general | solution.py:94
  39.0 1.0 %convolution_multiply_fusion = f32[512,512]{0,1:T(8,128)S(1)} fusion(f32[33,512]{1,0:T(8,128)S(1)} %collective-permute-done.3, f32[4,32,128]{2,1,0:T(8,128)S(1)} %gather_fusion), kind=kOutput, calls=%fused_computation.2 | convolution fusion | flops 100925440 | bytes 1179648 | tf_op jit(solution)/shard_map/dn,dp->np/dot_general | solution.py:32
  40.0 2.1 %multiply_reduce_fusion = (f32[512]{0:T(512)S(1)}, f32[512,512]{1,0:T(8,128)S(1)}) fusion(f32[512,512]{1,0:T(8,128)S(1)} %fusion.10, f32[512,512]{0,1:T(8,128)S(1)} %convolution_multiply_fusion, f32[512]{0:T(512)S(1)} %multiply_reduce_fusion.1, f32[512]{0:T(512)S(1)} %bitcast.103, pred[512]{0:T(512)(128)(4,1)S(1)} %add_compare_fusion, ...), kind=kOutput, calls=%fused_computation.19 | convolution fusion | flops 1612447232 | bytes 4200960 | tf_op jit(solution)/shard_map/dot_general | solution.py:95
  42.2 0.6 fusion.51
  42.8 0.1 collective-permute-start.4
  42.9 0.1 reshape.144
  43.0 1.1 %collective-permute-done.4 = f32[2,512]{1,0:T(2,128)S(1)} collective-permute-done((f32[2,512]{1,0:T(2,128)S(1)}, f32[2,512]{1,0:T(2,128)S(1)}, u32[]{:S(2)}, u32[]{:S(2)}) %collective-permute-start.4) | collective-permute-done | bytes 4128 | tf_op jit(solution)/shard_map/ppermute | solution.py:28
  44.1 0.3 convolution_reduce_fusion
  44.3 0.3 convolution_reduce_fusion.1
  44.6 0.6 pad_maximum_fusion.2
  45.2 3.2 %all-to-all-start = ((f32[4,2,128]{2,1,0:T(2,128)}), f32[4,2,128]{2,1,0:T(2,128)S(1)}, u32[]{:S(2)}, u32[]{:S(2)}) async-start(f32[4,2,128]{2,1,0:T(2,128)} %pad_maximum_fusion.2), calls=%async_computation | async-start | bytes 8192 | tf_op jit(solution)/shard_map/all_to_all | solution.py:118
  48.4 0.8 %dynamic-slice_convert_fusion = f32[4,1,4]{2,1,0:T(1,128)S(1)} fusion(s32[4,4,16]{2,1,0:T(4,128)} %param.10, s32[]{:T(128)S(6)} %select_n.84, s32[]{:T(128)S(6)} %select_n.86), kind=kLoop, calls=%fused_computation.70 | loop fusion | flops 16 | bytes 136 | tf_op jit(solution)/shard_map/convert_element_type | solution.py:119
  49.2 4.8 %all-to-all-done = f32[4,2,128]{2,1,0:T(2,128)S(1)} async-done(((f32[4,2,128]{2,1,0:T(2,128)}), f32[4,2,128]{2,1,0:T(2,128)S(1)}, u32[]{:S(2)}, u32[]{:S(2)}) %all-to-all-start) | async-done | bytes 4128 | tf_op jit(solution)/shard_map/all_to_all | solution.py:118
  54.0 0.2 convolution_bitcast_fusion
  54.2 12.8 %all-reduce = (f32[4,128]{1,0:T(4,128)S(1)}, f32[4,128]{1,0:T(4,128)S(1)}) all-reduce(f32[4,128]{1,0:T(4,128)S(1)} %get-tuple-element.9, f32[4,128]{1,0:T(4,128)S(1)} %get-tuple-element.8), channel_id=1, replica_groups=mesh['row'=4,'col'=8] {'col'}, use_global_device_ids=true, to_apply=%region_8.9 | all-reduce | flops 1024 | bytes 8192 | tf_op jit(solution)/shard_map/psum | solution.py:120
  67.0 0.6 add_divide_fusion
  (27 shorter events, 0.2 us)
Async XLA Ops:
  0.6 16.6 %copy-start = (s32[1,4]{1,0:T(1,128)S(1)}, s32[1,4]{1,0:T(1,128)}, u32[]{:S(2)}) copy-start(s32[1,4]{1,0:T(1,128)} %param.9) | copy-start | bytes 52
  0.6 22.1 %collective-permute-start = (f32[4,32,128]{2,1,0:T(8,128)}, f32[4,32,128]{2,1,0:T(8,128)S(1)}, u32[]{:S(2)}, u32[]{:S(2)}) collective-permute-start(f32[4,32,128]{2,1,0:T(8,128)} %param.11), channel_id=1, source_target_pairs={{0,8},{8,16},{16,24},{24,0},{1,9},{9,17},{17,25},{25,1},{2,10},{10... | collective-permute-start | bytes 196616 | tf_op jit(solution)/shard_map/ppermute | solution.py:15
  4.6 19.8 %collective-permute-start.3 = (f32[33,512]{1,0:T(8,128)S(1)}, f32[33,512]{1,0:T(8,128)S(1)}, u32[]{:S(2)}, u32[]{:S(2)}) collective-permute-start(f32[33,512]{1,0:T(8,128)S(1)} %pad_maximum_fusion), channel_id=1, source_target_pairs={{0,1},{1,0},{2,3},{3,2},{4,5},{5,4},{6,7},{7,6},{8,9},{9,8},{10,11... | collective-permute-start | bytes 202760 | tf_op jit(solution)/shard_map/ppermute | solution.py:28
  13.8 6.1 %copy-start.3 = (f32[1,512]{1,0:T(1,128)S(1)}, f32[1,512]{1,0:T(1,128)}, u32[]{:S(2)}) copy-start(f32[1,512]{1,0:T(1,128)} %param.7) | copy-start | bytes 6148
  18.5 16.7 %copy-start.2 = (f32[4,32,128]{2,1,0:T(8,128)S(1)}, f32[4,32,128]{2,1,0:T(8,128)}, u32[]{:S(2)}) copy-start(f32[4,32,128]{2,1,0:T(8,128)} %param.11) | copy-start | bytes 196612
  19.8 16.1 %copy-start.1 = (f32[1,32,512]{2,1,0:T(8,128)S(1)}, f32[1,32,512]{2,1,0:T(8,128)}, u32[]{:S(2)}) copy-start(f32[1,32,512]{2,1,0:T(8,128)} %param.6) | copy-start | bytes 196612
  22.8 6.3 %collective-permute-start.1 = (f32[4,32,128]{2,1,0:T(8,128)S(1)}, f32[4,32,128]{2,1,0:T(8,128)S(1)}, u32[]{:S(2)}, u32[]{:S(2)}) collective-permute-start(f32[4,32,128]{2,1,0:T(8,128)S(1)} %collective-permute-done), channel_id=1, source_target_pairs={{0,8},{8,16},{16,24},{24,0},{1,9},{9,17},{17,25},{25,1},{2,10},{10... | collective-permute-start | bytes 196616 | tf_op jit(solution)/shard_map/ppermute | solution.py:15
  29.1 6.1 %collective-permute-start.2 = (f32[4,32,128]{2,1,0:T(8,128)S(1)}, f32[4,32,128]{2,1,0:T(8,128)S(1)}, u32[]{:S(2)}, u32[]{:S(2)}) collective-permute-start(f32[4,32,128]{2,1,0:T(8,128)S(1)} %collective-permute-done.1), channel_id=1, source_target_pairs={{0,8},{8,16},{16,24},{24,0},{1,9},{9,17},{17,25},{25,1},{2,10},{10... | collective-permute-start | bytes 196616 | tf_op jit(solution)/shard_map/ppermute | solution.py:15
  42.8 1.2 %collective-permute-start.4 = (f32[2,512]{1,0:T(2,128)S(1)}, f32[2,512]{1,0:T(2,128)S(1)}, u32[]{:S(2)}, u32[]{:S(2)}) collective-permute-start(f32[2,512]{1,0:T(2,128)S(1)} %pad_maximum_fusion.1), channel_id=1, source_target_pairs={{0,1},{1,0},{2,3},{3,2},{4,5},{5,4},{6,7},{7,6},{8,9},{9,8},{10,11... | collective-permute-start | bytes 12296 | tf_op jit(solution)/shard_map/ppermute | solution.py:28
  45.2 8.8 %all-to-all-start = ((f32[4,2,128]{2,1,0:T(2,128)}), f32[4,2,128]{2,1,0:T(2,128)S(1)}, u32[]{:S(2)}, u32[]{:S(2)}) async-start(f32[4,2,128]{2,1,0:T(2,128)} %pad_maximum_fusion.2), calls=%async_computation | async-start | bytes 8192 | tf_op jit(solution)/shard_map/all_to_all | solution.py:118
